TPU v7x, 32 devices: a whole 2x2x4 slice. The times are simulated.
32 devices in a mesh: tok: 2 (over x), blk: 16 (over z, y, core).
Axes of the slice: x: 2, y: 2, z: 4, core: 2. Of those that a mesh axis runs over, the one named last changes fastest.
Arguments:
- grad_out: bfloat16 [2048, 8192], P('tok', 'blk'), may hold values from -6 to 6
- acts: bfloat16 [2048, 512], P('tok', 'blk'), may hold values from -6 to 6
- stat_old: float32 [2, 16, 512, 512], P('tok', 'blk'), may hold values from -1 to 6, as said below
- root_old: float32 [2, 16, 512, 512], P('tok', 'blk'), may hold values from -1 to 2, as said below
- assign: int32 [16, 2], P('blk'), may hold values from 0 to 1, as said below
Outputs:
- roots: float32 [2, 16, 512, 512], P('tok', 'blk')
- precond: float32 [2, 16, 256, 512], P('tok', 'blk')
Inputs may be any that keep to these rules, and one draw needn't show every extreme that they name: `assign`: row j gives each of its 2 slots a job 2 b + s with b < 1 and s in 0, 1; every job once in a row; slots 2 m and 2 m + 1 hold the two sides of one block. `stat_old`: each slot's matrix is symmetric and positive definite. `root_old`: each slot's matrix is symmetric.
All inputs are finite; a program needn't handle non-finite values.
Results may differ from a plain program's by a relative error of at most 0.0003.
Values may be sent and summed in bfloat16 or wider, within the bound.
No kernel may reach another device: no remote copies, remote signals or barrier semaphores. Data moves between devices by JAX's collectives and lax.ppermute only.
A program may use at most 64 MiB of HBM per device.

v0:
```python
import math

import jax
import jax.numpy as jnp
from jax import lax
from jax.sharding import PartitionSpec as P

ITERS = 2


BETA = 0.9
DAMPING = 0.001


def swapped(block, axis, stride):
    count = lax.axis_size(axis)
    route = []
    for low in range(count):
        high = low | 1 << stride
        if high != low and high < count:
            route += [(low, high), (high, low)]
    return lax.ppermute(block, axis, route)


def shortened(x):
    return jax.tree.map(lambda a: a.astype(jnp.bfloat16) if a.dtype == jnp.float32 else a, x)


def product(lhs_matrix, rhs_matrix):
    return jnp.dot(
        lhs_matrix, rhs_matrix, precision=lax.Precision.HIGHEST, preferred_element_type=jnp.float32
    )


def newton_root(statistic, warm_root, square):
    identity = jnp.eye(square.shape[0], dtype=jnp.float32)
    factor = BETA * statistic + (1.0 - BETA) * square + DAMPING * identity
    root_square = product(warm_root, warm_root)
    coupled = product(product(root_square, root_square), factor)
    current = warm_root
    for iteration in range(ITERS):
        update = (5.0 * identity - coupled) * 0.25
        current = product(current, update)
        if iteration + 1 < ITERS:
            update_square = product(update, update)
            coupled = product(product(update_square, update_square), coupled)
    return current


def block_partials(rows_part, cols_part, group_blocks, block_size, scaling):
    shaped = cols_part.reshape(cols_part.shape[0], group_blocks, block_size)
    return (
        jnp.einsum("tr,tgc->grc", rows_part, shaped, preferred_element_type=jnp.float32) * scaling
    )


def join_pair(mine, theirs, column, bit):
    lower = column // (1 << bit) % 2 == 0
    return jnp.where(
        lower, jnp.concatenate([mine, theirs], axis=1), jnp.concatenate([theirs, mine], axis=1)
    )


def shards(grad_out, acts, stat_old, root_old, assign):
    token_groups = lax.axis_size("tok")
    blk_count = lax.axis_size("blk")
    column = lax.axis_index("blk")
    position = lax.axis_index("tok")
    block_size = stat_old.shape[-1]
    shard_rows = grad_out.shape[0]
    all_tokens = shard_rows * token_groups
    scaling = 1.0 / math.sqrt(all_tokens)
    strips = grad_out.shape[1] * blk_count // block_size
    strip_bits = strips.bit_length() - 1
    blk_bits = blk_count.bit_length() - 1
    group_blocks = token_groups // 2
    cols_part = acts
    for bit in range(strip_bits):
        other_cols = swapped(cols_part, "blk", bit)
        cols_part = join_pair(cols_part, other_cols, column, bit)
    rows_part = grad_out
    for bit in range(strip_bits, blk_bits):
        other_rows = swapped(shortened(rows_part), "blk", bit).astype(rows_part.dtype)
        rows_part = join_pair(rows_part, other_rows, column, bit)
    job_table = assign[0]
    job_index = job_table[position]
    side_bit = job_index % 2
    partial_value = block_partials(rows_part, cols_part, group_blocks, block_size, scaling)
    halves = partial_value.reshape(group_blocks * 2, block_size // 2, block_size)[job_table]
    own_half = lax.psum_scatter(halves, "tok", scatter_dimension=0, tiled=True)[0]
    other_half = swapped(own_half, "tok", 0)
    chosen = jnp.where(
        side_bit == 0,
        jnp.concatenate([own_half, other_half], axis=0),
        jnp.concatenate([other_half, own_half], axis=0),
    )
    oriented = jnp.where(side_bit == 0, chosen, chosen.T)
    square = product(oriented, oriented.T) / all_tokens
    own_root = newton_root(stat_old[0, 0], root_old[0, 0], square)
    other_root = swapped(own_root, "tok", 0)
    left_root = jnp.where(side_bit == 0, own_root, other_root)
    right_root = jnp.where(side_bit == 0, other_root, own_root)
    half_rows = lax.dynamic_slice_in_dim(
        left_root, side_bit * (block_size // 2), block_size // 2, 0
    )
    precond = product(product(half_rows, chosen), right_root)
    return (own_root[None, None], precond[None, None])


def solution(mesh):
    placed = (
        P("tok", "blk"),
        P("tok", "blk"),
        P("tok", "blk", None, None),
        P("tok", "blk", None, None),
        P("blk", None),
    )
    return jax.shard_map(
        shards,
        mesh=mesh,
        in_specs=placed,
        out_specs=(P("tok", "blk", None, None), P("tok", "blk", None, None)),
        check_vma=False,
    )
```

profile of v0, /device:TPU:0, one launch (start us, length us, event | category | flops | bytes accessed | tf_op | source)
XLA Modules:
  0.0 145.0 jit_solution(18428726512472327188)
XLA Ops:
  7.2 0.0 copy-start
  7.2 0.0 copy-start.4
  7.2 0.0 reduce-scatter.2.cloned.1.call-start
  7.2 0.6 collective-permute-start
  7.8 1.1 collective-permute-done
  8.9 0.9 maximum_select_fusion.5
  9.9 2.9 %collective-permute-start.1 = (bf16[1024,64]{0,1:T(8,128)(2,1)S(1)}, bf16[1024,64]{0,1:T(8,128)(2,1)S(1)}, u32[]{:S(2)}, u32[]{:S(2)}) collective-permute-start(bf16[1024,64]{0,1:T(8,128)(2,1)S(1)} %maximum_select_fusion.5), channel_id=1, source_target_pairs={{0,2},{2,0},{1,3},{3,1},{4,6},{6,4},{5,7},{7,5},{8,10},{10,8},{9,1... | collective-permute-start | bytes 393224 | tf_op jit(solution)/shard_map/ppermute | solution.py:22
  12.8 3.8 %collective-permute-done.1 = bf16[1024,64]{0,1:T(8,128)(2,1)S(1)} collective-permute-done((bf16[1024,64]{0,1:T(8,128)(2,1)S(1)}, bf16[1024,64]{0,1:T(8,128)(2,1)S(1)}, u32[]{:S(2)}, u32[]{:S(2)}) %collective-permute-start.1) | collective-permute-done | bytes 131104 | tf_op jit(solution)/shard_map/ppermute | solution.py:22
  16.7 1.9 %collective-permute-start.2 = (bf16[1024,128]{0,1:T(8,128)(2,1)S(1)}, bf16[1024,128]{0,1:T(8,128)(2,1)S(1)}, u32[]{:S(2)}, u32[]{:S(2)}) collective-permute-start(bf16[1024,128]{0,1:T(8,128)(2,1)S(1)} %maximum_select_fusion.4), channel_id=1, source_target_pairs={{0,4},{4,0},{1,5},{5,1},{2,6},{6,2},{3,7},{7,3},{8,12},{12,8},{9,1... | collective-permute-start | bytes 786440 | tf_op jit(solution)/shard_map/ppermute | solution.py:22
  18.5 6.0 %collective-permute-done.2 = bf16[1024,128]{0,1:T(8,128)(2,1)S(1)} collective-permute-done((bf16[1024,128]{0,1:T(8,128)(2,1)S(1)}, bf16[1024,128]{0,1:T(8,128)(2,1)S(1)}, u32[]{:S(2)}, u32[]{:S(2)}) %collective-permute-start.2) | collective-permute-done | bytes 262176 | tf_op jit(solution)/shard_map/ppermute | solution.py:22
  24.5 0.1 maximum_select_fusion.3
  24.6 2.6 %collective-permute-start.3 = (bf16[1024,256]{0,1:T(8,128)(2,1)S(1)}, bf16[1024,256]{0,1:T(8,128)(2,1)}, u32[]{:S(2)}, u32[]{:S(2)}) collective-permute-start(bf16[1024,256]{0,1:T(8,128)(2,1)S(1)} %maximum_select_fusion.3), channel_id=1, source_target_pairs={{0,8},{8,0},{1,9},{9,1},{2,10},{10,2},{3,11},{11,3},{4,12},{12,4},... | collective-permute-start | bytes 1572872 | tf_op jit(solution)/shard_map/ppermute | solution.py:22
  27.2 0.0 copy-done.4
  27.3 22.2 %collective-permute-done.3 = bf16[1024,256]{0,1:T(8,128)(2,1)} collective-permute-done((bf16[1024,256]{0,1:T(8,128)(2,1)S(1)}, bf16[1024,256]{0,1:T(8,128)(2,1)}, u32[]{:S(2)}, u32[]{:S(2)}) %collective-permute-start.3) | collective-permute-done | bytes 524320 | tf_op jit(solution)/shard_map/ppermute | solution.py:22
  49.5 2.3 %convolution_multiply_fusion.1 = f32[512,512]{0,1:T(8,128)S(1)} fusion(bf16[1024,512]{1,0:T(8,128)(2,1)} %param.5, bf16[1024,256]{0,1:T(8,128)(2,1)} %collective-permute-done.3, bf16[1024,256]{0,1:T(8,128)(2,1)S(1)} %maximum_select_fusion.3, pred[]{:T(512)S(6)} %eq.33), kind=kOutput, calls=%fused_computation.5 | convolution fusion | flops 541851648 | bytes 3145729 | tf_op jit(solution)/shard_map/tr,tgc->grc/dot_general | solution.py:53
  51.8 0.6 gather_fusion
  52.4 1.3 copy.9
  53.8 0.0 reduce-scatter.2.cloned.1.call-update
  53.8 0.6 constant_dynamic-slice_fusion
  56.3 18.8 %reduce-scatter.2.cloned.1.call-done = f32[1,256,512]{1,2,0:T(8,128)} async-done(((f32[2,256,512]{1,2,0:T(8,128)}), f32[1,256,512]{1,2,0:T(8,128)}) %reduce-scatter.2.cloned.1.call-update) | async-done | bytes 524304 | tf_op jit(solution)/shard_map/reduce_scatter | solution.py:90
  75.1 0.3 collective-permute-start.4
  75.5 0.0 copy-done
  75.5 1.8 %fusion.11 = f32[512,512]{1,0:T(8,128)S(1)} fusion(f32[1,1,512,512]{3,2,1,0:T(8,128)S(1)} %copy-done), kind=kOutput, calls=%fused_computation.20 | convolution fusion | flops 1610612736 | bytes 2097152 | tf_op jit(solution)/shard_map/dot_general | solution.py:30
  77.3 0.0 copy-start.2
  77.3 1.8 %fusion.38 = f32[512,512]{1,0:T(8,128)S(1)} fusion(f32[512,512]{1,0:T(8,128)S(1)} %fusion.11), kind=kOutput, calls=%fused_computation.53 | convolution fusion | flops 1610612736 | bytes 2097152 | tf_op jit(solution)/shard_map/dot_general | solution.py:30
  79.2 9.6 %collective-permute-done.4 = f32[256,512]{0,1:T(8,128)S(1)} collective-permute-done((f32[256,512]{0,1:T(8,128)}, f32[256,512]{0,1:T(8,128)S(1)}, u32[]{:S(2)}, u32[]{:S(2)}) %collective-permute-start.4) | collective-permute-done | bytes 524320 | tf_op jit(solution)/shard_map/ppermute | solution.py:22
  88.8 0.0 copy-start.3
  88.8 0.8 copy-done.3
  89.6 0.0 copy-done.2
  89.6 0.2 maximum_select_fusion.2
  89.8 1.3 copy.11
  91.1 5.0 %fusion.1 = f32[512,512]{1,0:T(8,128)S(1)} fusion(f32[512,512]{1,0:T(8,128)} %copy.11, f32[1,1,512,512]{3,2,1,0:T(8,128)} %param.7, pred[]{:T(512)S(6)} %eq.32, f32[256,512]{0,1:T(8,128)} %copy-done.3, f32[256,512]{0,1:T(8,128)} %bitcast.39), kind=kOutput, calls=%fused_computation.6 | convolution fusion | flops 1613234176 | bytes 4194305 | tf_op jit(solution)/shard_map/dot_general | solution.py:30
  96.0 1.8 %fusion.39 = f32[512,512]{1,0:T(8,128)S(1)} fusion(f32[512,512]{1,0:T(8,128)S(1)} %fusion.38, f32[512,512]{1,0:T(8,128)S(1)} %fusion.1), kind=kOutput, calls=%fused_computation.54 | convolution fusion | flops 1610612736 | bytes 3145728 | tf_op jit(solution)/shard_map/dot_general | solution.py:30
  97.9 1.9 %fusion.15 = f32[512,512]{1,0:T(8,128)S(1)} fusion(f32[512,512]{1,0:T(8,128)S(1)} %fusion.39), kind=kOutput, calls=%fused_computation.25 | convolution fusion | flops 1611661312 | bytes 2097152 | tf_op jit(solution)/shard_map/dot_general | solution.py:30
  99.8 3.7 %fusion.9 = f32[512,512]{1,0:T(8,128)S(1)} fusion(f32[1,1,512,512]{3,2,1,0:T(8,128)S(1)} %copy-done, f32[512,512]{1,0:T(8,128)S(1)} %fusion.39), kind=kOutput, calls=%fused_computation.18 | convolution fusion | flops 1611661312 | bytes 3145728 | tf_op jit(solution)/shard_map/dot_general | solution.py:30
  103.5 1.8 %fusion.40 = f32[512,512]{1,0:T(8,128)S(1)} fusion(f32[512,512]{1,0:T(8,128)S(1)} %fusion.15), kind=kOutput, calls=%fused_computation.55 | convolution fusion | flops 1610612736 | bytes 2097152 | tf_op jit(solution)/shard_map/dot_general | solution.py:30
  105.3 1.9 %fusion.2 = f32[512,512]{1,0:T(8,128)S(1)} fusion(f32[512,512]{1,0:T(8,128)S(1)} %fusion.40, f32[512,512]{1,0:T(8,128)S(1)} %fusion.39), kind=kOutput, calls=%fused_computation.7 | convolution fusion | flops 1611661312 | bytes 3145728 | tf_op jit(solution)/shard_map/dot_general | solution.py:30
  107.2 1.8 %fusion.41 = f32[512,512]{1,0:T(8,128)S(1)} fusion(f32[512,512]{1,0:T(8,128)S(1)} %fusion.9, f32[512,512]{1,0:T(8,128)S(1)} %fusion.2), kind=kOutput, calls=%fused_computation.56 | convolution fusion | flops 1610612736 | bytes 3145728 | tf_op jit(solution)/shard_map/dot_general | solution.py:30
  109.1 0.0 copy-start.1
  109.1 1.2 collective-permute-start.5
  110.3 23.3 %collective-permute-done.5 = f32[512,512]{1,0:T(8,128)S(1)} collective-permute-done((f32[512,512]{1,0:T(8,128)S(1)}, f32[512,512]{1,0:T(8,128)S(1)}, u32[]{:S(2)}, u32[]{:S(2)}) %collective-permute-start.5) | collective-permute-done | bytes 1048608 | tf_op jit(solution)/shard_map/ppermute | solution.py:22
  133.6 2.7 %fusion.18 = f32[256,512]{1,0:T(8,128)S(1)} fusion(f32[512,512]{1,0:T(8,128)S(1)} %collective-permute-done.5, s32[]{:T(128)S(6)} %select_n.126, f32[512,512]{1,0:T(8,128)S(1)} %fusion.41, pred[]{:T(512)S(6)} %eq.32, f32[256,512]{0,1:T(8,128)} %copy-done.3, f32[256,512]{0,1:T(8,128)} %bitcast.40), kind=kOutput, calls=%fused_computation.27 | convolution fusion | flops 806223872 | bytes 2622976 | tf_op jit(solution)/shard_map/dot_general | solution.py:30
  136.2 0.0 copy-done.1
  136.2 1.9 %convolution_bitcast_fusion = f32[1,1,256,512]{3,2,1,0:T(8,128)} fusion(f32[256,512]{1,0:T(8,128)S(1)} %fusion.18, f32[512,512]{1,0:T(8,128)S(1)} %collective-permute-done.5, f32[512,512]{1,0:T(8,128)S(1)} %fusion.41, pred[]{:T(512)S(6)} %eq.32), kind=kOutput, calls=%fused_computation.8 | convolution fusion | flops 805568512 | bytes 3145729 | tf_op jit(solution)/shard_map/dot_general | solution.py:30
  (3 shorter events, 0.1 us)
Async XLA Ops:
  7.2 68.3 %copy-start = (f32[1,1,512,512]{3,2,1,0:T(8,128)S(1)}, f32[1,1,512,512]{3,2,1,0:T(8,128)}, u32[]{:S(2)}) copy-start(f32[1,1,512,512]{3,2,1,0:T(8,128)} %param.8) | copy-start | bytes 3145732
  7.2 20.1 %copy-start.4 = (s32[1,2]{1,0:T(1,128)S(1)}, s32[1,2]{1,0:T(1,128)}, u32[]{:S(2)}) copy-start(s32[1,2]{1,0:T(1,128)} %param.9) | copy-start | bytes 28
  7.2 67.9 %reduce-scatter.2.cloned.1.call-start = ((), (), s32[]{:S(2)}) async-start(), calls=%async_computation.1 | async-start | bytes 1572864 | tf_op jit(solution)/shard_map/reduce_scatter | solution.py:90
  7.2 1.7 %collective-permute-start = (bf16[1024,32]{0,1:T(8,128)(2,1)}, bf16[1024,32]{0,1:T(8,128)(2,1)S(1)}, u32[]{:S(2)}, u32[]{:S(2)}) collective-permute-start(bf16[1024,32]{0,1:T(8,128)(2,1)} %param.6), channel_id=1, source_target_pairs={{0,1},{1,0},{2,3},{3,2},{4,5},{5,4},{6,7},{7,6},{8,9},{9,8},{10,11... | collective-permute-start | bytes 196616 | tf_op jit(solution)/shard_map/ppermute | solution.py:22
  9.9 6.7 %collective-permute-start.1 = (bf16[1024,64]{0,1:T(8,128)(2,1)S(1)}, bf16[1024,64]{0,1:T(8,128)(2,1)S(1)}, u32[]{:S(2)}, u32[]{:S(2)}) collective-permute-start(bf16[1024,64]{0,1:T(8,128)(2,1)S(1)} %maximum_select_fusion.5), channel_id=1, source_target_pairs={{0,2},{2,0},{1,3},{3,1},{4,6},{6,4},{5,7},{7,5},{8,10},{10,8},{9,1... | collective-permute-start | bytes 393224 | tf_op jit(solution)/shard_map/ppermute | solution.py:22
  16.7 7.9 %collective-permute-start.2 = (bf16[1024,128]{0,1:T(8,128)(2,1)S(1)}, bf16[1024,128]{0,1:T(8,128)(2,1)S(1)}, u32[]{:S(2)}, u32[]{:S(2)}) collective-permute-start(bf16[1024,128]{0,1:T(8,128)(2,1)S(1)} %maximum_select_fusion.4), channel_id=1, source_target_pairs={{0,4},{4,0},{1,5},{5,1},{2,6},{6,2},{3,7},{7,3},{8,12},{12,8},{9,1... | collective-permute-start | bytes 786440 | tf_op jit(solution)/shard_map/ppermute | solution.py:22
  24.6 24.9 %collective-permute-start.3 = (bf16[1024,256]{0,1:T(8,128)(2,1)S(1)}, bf16[1024,256]{0,1:T(8,128)(2,1)}, u32[]{:S(2)}, u32[]{:S(2)}) collective-permute-start(bf16[1024,256]{0,1:T(8,128)(2,1)S(1)} %maximum_select_fusion.3), channel_id=1, source_target_pairs={{0,8},{8,0},{1,9},{9,1},{2,10},{10,2},{3,11},{11,3},{4,12},{12,4},... | collective-permute-start | bytes 1572872 | tf_op jit(solution)/shard_map/ppermute | solution.py:22
  75.1 13.7 %collective-permute-start.4 = (f32[256,512]{0,1:T(8,128)}, f32[256,512]{0,1:T(8,128)S(1)}, u32[]{:S(2)}, u32[]{:S(2)}) collective-permute-start(f32[256,512]{0,1:T(8,128)} %bitcast.38), channel_id=1, source_target_pairs={{0,16},{16,0},{1,17},{17,1},{2,18},{18,2},{3,19},{19,3},{4,20},{20... | collective-permute-start | bytes 1572872 | tf_op jit(solution)/shard_map/ppermute | solution.py:22
  77.3 12.3 %copy-start.2 = (f32[1,256,512]{1,2,0:T(8,128)S(1)}, f32[1,256,512]{1,2,0:T(8,128)}, u32[]{:S(2)}) copy-start(f32[1,256,512]{1,2,0:T(8,128)} %reduce-scatter.2.cloned.1.call-done) | copy-start | bytes 1572868
  88.8 0.8 copy-start.3
  109.1 27.2 %copy-start.1 = (f32[512,512]{1,0:T(8,128)}, f32[512,512]{1,0:T(8,128)S(1)}, u32[]{:S(2)}) copy-start(f32[512,512]{1,0:T(8,128)S(1)} %fusion.41) | copy-start | bytes 3145732
  109.1 24.5 %collective-permute-start.5 = (f32[512,512]{1,0:T(8,128)S(1)}, f32[512,512]{1,0:T(8,128)S(1)}, u32[]{:S(2)}, u32[]{:S(2)}) collective-permute-start(f32[512,512]{1,0:T(8,128)S(1)} %fusion.41), channel_id=1, source_target_pairs={{0,16},{16,0},{1,17},{17,1},{2,18},{18,2},{3,19},{19,3},{4,20},{20... | collective-permute-start | bytes 3145736 | tf_op jit(solution)/shard_map/ppermute | solution.py:22
Sparse Core Ops, SparseCore 0:
  53.9 21.1 reduce-scatter.1
where the time goes:
time: 145 us
  waiting for transfers between devices  84.9 us (59%)
  matrix products  28.5 us (20%)
  between operations  16.2 us (11%)
  starting transfers between devices  9.51 us (7%)
  local copies, waits for them, and re-layouts  4.63 us (3%)
    ppermute x6, waiting for transfers between devices, swapped(): return lax.ppermute(block, axis, route)  66.1 us
    dot_general x11, matrix products, product(): jnp.dot(lhs_matrix, rhs_matrix, precision=lax.Precision.HIGHEST, preferre...  26.1 us
    reduce_scatter x1, waiting for transfers between devices, shards(): lax.psum_scatter(halves, 'tok', scatter_dimension=0, tiled=True)[0]  18.8 us
    ppermute x6, starting transfers between devices, swapped(): return lax.ppermute(block, axis, route)  9.47 us
  transfers between devices with their start and end apart: 7, of which 7 were waited for; matrix products, arithmetic and copies ran while one was open for 3% of the time, Pallas kernels for 0%

commit v1 on v0

--- a/solution.py
+++ b/solution.py
@@ -28,7 +28,7 @@
 
 def product(lhs_matrix, rhs_matrix):
     return jnp.dot(
-        lhs_matrix, rhs_matrix, precision=lax.Precision.HIGHEST, preferred_element_type=jnp.float32
+        lhs_matrix, rhs_matrix, precision=lax.Precision.HIGH, preferred_element_type=jnp.float32
     )
 
 
@@ -57,7 +57,7 @@
 def join_pair(mine, theirs, column, bit):
     lower = column // (1 << bit) % 2 == 0
     return jnp.where(
-        lower, jnp.concatenate([mine, theirs], axis=1), jnp.concatenate([theirs, mine], axis=1)
+        lower, jnp.concatenate([mine, theirs], axis=0), jnp.concatenate([theirs, mine], axis=0)
     )
 
 
@@ -74,26 +74,32 @@
     strip_bits = strips.bit_length() - 1
     blk_bits = blk_count.bit_length() - 1
     group_blocks = token_groups // 2
-    cols_part = acts
-    for bit in range(strip_bits):
+    cols_part = acts.T
+    for bit in reversed(range(strip_bits)):
         other_cols = swapped(cols_part, "blk", bit)
         cols_part = join_pair(cols_part, other_cols, column, bit)
+    cols_part = cols_part.reshape((2,) * strip_bits + acts.shape[::-1])
+    cols_part = cols_part.transpose(tuple(reversed(range(strip_bits))) + (strip_bits, strip_bits + 1))
+    cols_part = cols_part.reshape(-1, shard_rows).T
     rows_part = grad_out
     for bit in range(strip_bits, blk_bits):
         other_rows = swapped(shortened(rows_part), "blk", bit).astype(rows_part.dtype)
-        rows_part = join_pair(rows_part, other_rows, column, bit)
+        rows_part = join_pair(rows_part.T, other_rows.T, column, bit).T
     job_table = assign[0]
     job_index = job_table[position]
     side_bit = job_index % 2
     partial_value = block_partials(rows_part, cols_part, group_blocks, block_size, scaling)
-    halves = partial_value.reshape(group_blocks * 2, block_size // 2, block_size)[job_table]
-    own_half = lax.psum_scatter(halves, "tok", scatter_dimension=0, tiled=True)[0]
-    other_half = swapped(own_half, "tok", 0)
-    chosen = jnp.where(
-        side_bit == 0,
-        jnp.concatenate([own_half, other_half], axis=0),
-        jnp.concatenate([other_half, own_half], axis=0),
-    )
+    if token_groups == 2:
+        chosen = (partial_value + swapped(partial_value, "tok", 0))[0]
+    else:
+        halves = partial_value.reshape(group_blocks * 2, block_size // 2, block_size)[job_table]
+        own_half = lax.psum_scatter(halves, "tok", scatter_dimension=0, tiled=True)[0]
+        other_half = swapped(own_half, "tok", 0)
+        chosen = jnp.where(
+            side_bit == 0,
+            jnp.concatenate([own_half, other_half], axis=0),
+            jnp.concatenate([other_half, own_half], axis=0),
+        )
     oriented = jnp.where(side_bit == 0, chosen, chosen.T)
     square = product(oriented, oriented.T) / all_tokens
     own_root = newton_root(stat_old[0, 0], root_old[0, 0], square)

time: 145 us -> 95.9 us (0.66)
  waiting for transfers between devices: 84.9 us -> 56.4 us
  between operations: 16.2 us -> 2.78 us
  matrix products: 28.5 us -> 18.4 us
  other arithmetic: 1.28 us -> 3.35 us
    reduce_scatter x1 -> x0, waiting for transfers between devices: 18.8 us -> none  [shards(): lax.psum_scatter(halves, 'tok', scatter_dimension=0, tiled=True)[0]]
    ppermute x6, waiting for transfers between devices: 66.1 us -> 56.4 us  [swapped(): return lax.ppermute(block, axis, route)]
    dot_general x11, matrix products: 26.1 us -> 17.7 us  [product(): jnp.dot(lhs_matrix, rhs_matrix, precision=lax.Precision.HIGH, preferred_e...]
    gather x2 -> x0, local copies, waits for them, and re-layouts: 1.92 us -> none  [shards(): partial_value.reshape(group_blocks * 2, block_size // 2, block_size)]
    squeeze x0 -> x1, other arithmetic: none -> 1.75 us  [shards(): chosen = (partial_value + swapped(partial_value, 'tok', 0))[0]]
    dot_general x1, matrix products: 2.32 us -> 0.71 us  [block_partials(): jnp.einsum('tr,tgc->grc', rows_part, shaped, preferred_element_type=jnp.f...]
    dot_general x0 -> x1, local copies, waits for them, and re-layouts: none -> 1.55 us  [product(): jnp.dot(lhs_matrix, rhs_matrix, precision=lax.Precision.HIGH, preferred_e...]
  transfers between devices with their start and end apart: 7 -> 6, of which waited for: 7 -> 6; matrix products, arithmetic and copies ran while one was open for 3% -> 3% of each run, Pallas kernels for 0% -> 0%
where the time goes in v1:
time: 95.9 us
  waiting for transfers between devices  56.4 us (59%)
  matrix products  18.4 us (19%)
  starting transfers between devices  10.3 us (11%)
  local copies, waits for them, and re-layouts  4.68 us (5%)
  other arithmetic  3.35 us (3%)
  between operations  2.78 us (3%)
    ppermute x6, waiting for transfers between devices, swapped(): return lax.ppermute(block, axis, route)  56.4 us
    dot_general x11, matrix products, product(): jnp.dot(lhs_matrix, rhs_matrix, precision=lax.Precision.HIGH, preferred_e...  17.7 us
    ppermute x6, starting transfers between devices, swapped(): return lax.ppermute(block, axis, route)  10.3 us
  transfers between devices with their start and end apart: 6, of which 6 were waited for; matrix products, arithmetic and copies ran while one was open for 3% of the time, Pallas kernels for 0%

profile of v1, /device:TPU:0, one launch (start us, length us, event | category | flops | bytes accessed | tf_op | source)
XLA Modules:
  0.0 95.9 jit_solution(14787872994543564210)
XLA Ops:
  0.6 0.0 copy-start
  0.6 4.1 %collective-permute-start = (bf16[32,1024]{1,0:T(8,128)(2,1)}, bf16[32,1024]{1,0:T(8,128)(2,1)S(1)}, u32[]{:S(2)}, u32[]{:S(2)}) collective-permute-start(bf16[32,1024]{1,0:T(8,128)(2,1)} %bitcast.42), channel_id=1, source_target_pairs={{0,8},{8,0},{1,9},{9,1},{2,10},{10,2},{3,11},{11,3},{4,12},{12,4},... | collective-permute-start | bytes 196616 | tf_op jit(solution)/shard_map/ppermute | solution.py:22
  4.8 3.9 %collective-permute-done = bf16[32,1024]{1,0:T(8,128)(2,1)S(1)} collective-permute-done((bf16[32,1024]{1,0:T(8,128)(2,1)}, bf16[32,1024]{1,0:T(8,128)(2,1)S(1)}, u32[]{:S(2)}, u32[]{:S(2)}) %collective-permute-start) | collective-permute-done | bytes 65568 | tf_op jit(solution)/shard_map/ppermute | solution.py:22
  8.6 0.9 maximum_select_fusion.3
  9.6 0.7 collective-permute-start.1
  10.3 4.3 %collective-permute-done.1 = bf16[64,1024]{1,0:T(8,128)(2,1)S(1)} collective-permute-done((bf16[64,1024]{1,0:T(8,128)(2,1)S(1)}, bf16[64,1024]{1,0:T(8,128)(2,1)S(1)}, u32[]{:S(2)}, u32[]{:S(2)}) %collective-permute-start.1) | collective-permute-done | bytes 131104 | tf_op jit(solution)/shard_map/ppermute | solution.py:22
  14.7 1.8 %collective-permute-start.2 = (bf16[128,1024]{1,0:T(8,128)(2,1)S(1)}, bf16[128,1024]{1,0:T(8,128)(2,1)S(1)}, u32[]{:S(2)}, u32[]{:S(2)}) collective-permute-start(bf16[128,1024]{1,0:T(8,128)(2,1)S(1)} %maximum_select_fusion.2), channel_id=1, source_target_pairs={{0,2},{2,0},{1,3},{3,1},{4,6},{6,4},{5,7},{7,5},{8,10},{10,8},{9,1... | collective-permute-start | bytes 786440 | tf_op jit(solution)/shard_map/ppermute | solution.py:22
  16.5 4.6 %collective-permute-done.2 = bf16[128,1024]{1,0:T(8,128)(2,1)S(1)} collective-permute-done((bf16[128,1024]{1,0:T(8,128)(2,1)S(1)}, bf16[128,1024]{1,0:T(8,128)(2,1)S(1)}, u32[]{:S(2)}, u32[]{:S(2)}) %collective-permute-start.2) | collective-permute-done | bytes 262176 | tf_op jit(solution)/shard_map/ppermute | solution.py:22
  21.1 0.1 maximum_select_fusion.1
  21.2 0.1 collective-permute-start.3
  21.3 1.9 %collective-permute-done.3 = bf16[256,1024]{1,0:T(8,128)(2,1)S(1)} collective-permute-done((bf16[256,1024]{1,0:T(8,128)(2,1)S(1)}, bf16[256,1024]{1,0:T(8,128)(2,1)S(1)}, u32[]{:S(2)}, u32[]{:S(2)}) %collective-permute-start.3) | collective-permute-done | bytes 524320 | tf_op jit(solution)/shard_map/ppermute | solution.py:22
  23.2 0.5 maximum_select_fusion
  23.7 0.0 copy-start.2
  23.7 0.1 copy.15
  23.8 1.1 %copy-done.2 = bf16[1024,512]{1,0:T(8,128)(2,1)S(1)} copy-done((bf16[1024,512]{1,0:T(8,128)(2,1)S(1)}, bf16[1024,512]{1,0:T(8,128)(2,1)}, u32[]{:S(2)}) %copy-start.2) | copy-done | bytes 1048600
  24.9 0.0 copy-start.3
  24.9 0.7 fusion.1
  25.7 0.0 copy-start.1
  25.7 1.8 %collective-permute-start.4 = (f32[1,512,512]{1,2,0:T(8,128)S(1)}, f32[1,512,512]{1,2,0:T(8,128)}, u32[]{:S(2)}, u32[]{:S(2)}) collective-permute-start(f32[1,512,512]{1,2,0:T(8,128)S(1)} %fusion.1), channel_id=1, source_target_pairs={{0,16},{16,0},{1,17},{17,1},{2,18},{18,2},{3,19},{19,3},{4,20},{20... | collective-permute-start | bytes 3145736 | tf_op jit(solution)/shard_map/ppermute | solution.py:22
  27.4 0.0 copy-done.3
  27.4 0.6 constant_dynamic-slice_fusion
  30.0 0.0 copy-done
  30.0 1.0 %fusion.7 = f32[512,512]{1,0:T(8,128)S(1)} fusion(f32[1,1,512,512]{3,2,1,0:T(8,128)S(1)} %copy-done), kind=kOutput, calls=%fused_computation.14 | convolution fusion | flops 805306368 | bytes 2097152 | tf_op jit(solution)/shard_map/dot_general | solution.py:30
  31.0 0.0 copy-done.1
  31.0 1.0 %fusion.31 = f32[512,512]{1,0:T(8,128)S(1)} fusion(f32[512,512]{1,0:T(8,128)S(1)} %fusion.7), kind=kOutput, calls=%fused_computation.43 | convolution fusion | flops 805306368 | bytes 2097152 | tf_op jit(solution)/shard_map/dot_general | solution.py:30
  32.0 19.0 %collective-permute-done.4 = f32[1,512,512]{1,2,0:T(8,128)} collective-permute-done((f32[1,512,512]{1,2,0:T(8,128)S(1)}, f32[1,512,512]{1,2,0:T(8,128)}, u32[]{:S(2)}, u32[]{:S(2)}) %collective-permute-start.4) | collective-permute-done | bytes 1048608 | tf_op jit(solution)/shard_map/ppermute | solution.py:22
  51.0 1.7 %add_bitcast_fusion = f32[512,512]{0,1:T(8,128)S(1)} fusion(f32[1,512,512]{1,2,0:T(8,128)} %copy-done.1, f32[1,512,512]{1,2,0:T(8,128)} %collective-permute-done.4), kind=kLoop, calls=%fused_computation.17 | loop fusion | flops 262144 | bytes 3145728 | tf_op jit(solution)/shard_map/squeeze | solution.py:93
  52.8 1.3 %copy.16 = f32[512,512]{1,0:T(8,128)} copy(f32[512,512]{0,1:T(8,128)S(1)} %add_bitcast_fusion) | data formatting | bytes 2097152 | tf_op jit(solution)/shard_map/squeeze | solution.py:93
  54.1 3.0 %fusion.2 = f32[512,512]{1,0:T(8,128)S(1)} fusion(f32[512,512]{0,1:T(8,128)S(1)} %add_bitcast_fusion, f32[512,512]{1,0:T(8,128)} %copy.16, f32[1,1,512,512]{3,2,1,0:T(8,128)} %param.7, pred[]{:T(512)S(6)} %eq.31), kind=kOutput, calls=%fused_computation.6 | convolution fusion | flops 807141376 | bytes 4194305 | tf_op jit(solution)/shard_map/dot_general | solution.py:30
  57.1 1.0 %fusion.32 = f32[512,512]{1,0:T(8,128)S(1)} fusion(f32[512,512]{1,0:T(8,128)S(1)} %fusion.31, f32[512,512]{1,0:T(8,128)S(1)} %fusion.2), kind=kOutput, calls=%fused_computation.44 | convolution fusion | flops 805306368 | bytes 3145728 | tf_op jit(solution)/shard_map/dot_general | solution.py:30
  58.1 1.0 %fusion.10 = f32[512,512]{1,0:T(8,128)S(1)} fusion(f32[512,512]{1,0:T(8,128)S(1)} %fusion.32), kind=kOutput, calls=%fused_computation.19 | convolution fusion | flops 806354944 | bytes 2097152 | tf_op jit(solution)/shard_map/dot_general | solution.py:30
  59.2 1.9 %fusion.5 = f32[512,512]{1,0:T(8,128)S(1)} fusion(f32[1,1,512,512]{3,2,1,0:T(8,128)S(1)} %copy-done, f32[512,512]{1,0:T(8,128)S(1)} %fusion.32), kind=kOutput, calls=%fused_computation.12 | convolution fusion | flops 806354944 | bytes 3145728 | tf_op jit(solution)/shard_map/dot_general | solution.py:30
  61.1 1.0 %fusion.33 = f32[512,512]{1,0:T(8,128)S(1)} fusion(f32[512,512]{1,0:T(8,128)S(1)} %fusion.10), kind=kOutput, calls=%fused_computation.45 | convolution fusion | flops 805306368 | bytes 2097152 | tf_op jit(solution)/shard_map/dot_general | solution.py:30
  62.1 1.0 %fusion.3 = f32[512,512]{1,0:T(8,128)S(1)} fusion(f32[512,512]{1,0:T(8,128)S(1)} %fusion.33, f32[512,512]{1,0:T(8,128)S(1)} %fusion.32), kind=kOutput, calls=%fused_computation.7 | convolution fusion | flops 806354944 | bytes 3145728 | tf_op jit(solution)/shard_map/dot_general | solution.py:30
  63.1 2.0 %fusion.34 = f32[512,512]{1,0:T(8,128)} fusion(f32[512,512]{1,0:T(8,128)S(1)} %fusion.5, f32[512,512]{1,0:T(8,128)S(1)} %fusion.3), kind=kOutput, calls=%fused_computation.46 | convolution fusion | flops 805306368 | bytes 3145728 | tf_op jit(solution)/shard_map/dot_general | solution.py:30
  65.1 1.6 %copy.18 = f32[512,512]{0,1:T(8,128)S(1)} copy(f32[512,512]{1,0:T(8,128)} %fusion.34) | data formatting | bytes 2097152 | tf_op jit(solution)/shard_map/dot_general | solution.py:30
  66.7 1.8 %collective-permute-start.5 = (f32[512,512]{0,1:T(8,128)S(1)}, f32[512,512]{0,1:T(8,128)}, u32[]{:S(2)}, u32[]{:S(2)}) collective-permute-start(f32[512,512]{0,1:T(8,128)S(1)} %copy.18), channel_id=1, source_target_pairs={{0,16},{16,0},{1,17},{17,1},{2,18},{18,2},{3,19},{19,3},{4,20},{20... | collective-permute-start | bytes 3145736 | tf_op jit(solution)/shard_map/ppermute | solution.py:22
  68.4 22.7 %collective-permute-done.5 = f32[512,512]{0,1:T(8,128)} collective-permute-done((f32[512,512]{0,1:T(8,128)S(1)}, f32[512,512]{0,1:T(8,128)}, u32[]{:S(2)}, u32[]{:S(2)}) %collective-permute-start.5) | collective-permute-done | bytes 1048608 | tf_op jit(solution)/shard_map/ppermute | solution.py:22
  91.2 2.1 %fusion.13 = f32[256,512]{1,0:T(8,128)S(1)} fusion(f32[512,512]{0,1:T(8,128)S(1)} %add_bitcast_fusion, f32[512,512]{0,1:T(8,128)} %collective-permute-done.5, s32[]{:T(128)S(6)} %select_n.113, f32[512,512]{0,1:T(8,128)S(1)} %copy.18, pred[]{:T(512)S(6)} %eq.31), kind=kOutput, calls=%fused_computation.21 | convolution fusion | flops 402784256 | bytes 2621445 | tf_op jit(solution)/shard_map/dot_general | solution.py:30
  93.3 2.7 %convolution_bitcast_fusion = f32[1,1,256,512]{3,2,1,0:T(8,128)} fusion(f32[256,512]{1,0:T(8,128)S(1)} %fusion.13, f32[512,512]{0,1:T(8,128)} %collective-permute-done.5, f32[512,512]{0,1:T(8,128)S(1)} %copy.18, pred[]{:T(512)S(6)} %eq.31), kind=kOutput, calls=%fused_computation.8 | convolution fusion | flops 402915328 | bytes 3145729 | tf_op jit(solution)/shard_map/dot_general | solution.py:30
  (1 shorter events, 0.0 us)
Async XLA Ops:
  0.6 29.3 %copy-start = (f32[1,1,512,512]{3,2,1,0:T(8,128)S(1)}, f32[1,1,512,512]{3,2,1,0:T(8,128)}, u32[]{:S(2)}) copy-start(f32[1,1,512,512]{3,2,1,0:T(8,128)} %param.8) | copy-start | bytes 3145732
  0.6 8.0 %collective-permute-start = (bf16[32,1024]{1,0:T(8,128)(2,1)}, bf16[32,1024]{1,0:T(8,128)(2,1)S(1)}, u32[]{:S(2)}, u32[]{:S(2)}) collective-permute-start(bf16[32,1024]{1,0:T(8,128)(2,1)} %bitcast.42), channel_id=1, source_target_pairs={{0,8},{8,0},{1,9},{9,1},{2,10},{10,2},{3,11},{11,3},{4,12},{12,4},... | collective-permute-start | bytes 196616 | tf_op jit(solution)/shard_map/ppermute | solution.py:22
  9.6 5.0 %collective-permute-start.1 = (bf16[64,1024]{1,0:T(8,128)(2,1)S(1)}, bf16[64,1024]{1,0:T(8,128)(2,1)S(1)}, u32[]{:S(2)}, u32[]{:S(2)}) collective-permute-start(bf16[64,1024]{1,0:T(8,128)(2,1)S(1)} %maximum_select_fusion.3), channel_id=1, source_target_pairs={{0,4},{4,0},{1,5},{5,1},{2,6},{6,2},{3,7},{7,3},{8,12},{12,8},{9,1... | collective-permute-start | bytes 393224 | tf_op jit(solution)/shard_map/ppermute | solution.py:22
  14.7 6.4 %collective-permute-start.2 = (bf16[128,1024]{1,0:T(8,128)(2,1)S(1)}, bf16[128,1024]{1,0:T(8,128)(2,1)S(1)}, u32[]{:S(2)}, u32[]{:S(2)}) collective-permute-start(bf16[128,1024]{1,0:T(8,128)(2,1)S(1)} %maximum_select_fusion.2), channel_id=1, source_target_pairs={{0,2},{2,0},{1,3},{3,1},{4,6},{6,4},{5,7},{7,5},{8,10},{10,8},{9,1... | collective-permute-start | bytes 786440 | tf_op jit(solution)/shard_map/ppermute | solution.py:22
  21.2 2.0 %collective-permute-start.3 = (bf16[256,1024]{1,0:T(8,128)(2,1)S(1)}, bf16[256,1024]{1,0:T(8,128)(2,1)S(1)}, u32[]{:S(2)}, u32[]{:S(2)}) collective-permute-start(bf16[256,1024]{1,0:T(8,128)(2,1)S(1)} %maximum_select_fusion.1), channel_id=1, source_target_pairs={{0,1},{1,0},{2,3},{3,2},{4,5},{5,4},{6,7},{7,6},{8,9},{9,8},{10,11... | collective-permute-start | bytes 1572872 | tf_op jit(solution)/shard_map/ppermute | solution.py:22
  23.7 1.2 %copy-start.2 = (bf16[1024,512]{1,0:T(8,128)(2,1)S(1)}, bf16[1024,512]{1,0:T(8,128)(2,1)}, u32[]{:S(2)}) copy-start(bf16[1024,512]{1,0:T(8,128)(2,1)} %param.5) | copy-start | bytes 3145732
  24.9 2.5 %copy-start.3 = (s32[1,2]{1,0:T(1,128)S(1)}, s32[1,2]{1,0:T(1,128)}, u32[]{:S(2)}) copy-start(s32[1,2]{1,0:T(1,128)} %param.9) | copy-start | bytes 28
  25.7 5.3 %copy-start.1 = (f32[1,512,512]{1,2,0:T(8,128)}, f32[1,512,512]{1,2,0:T(8,128)S(1)}, u32[]{:S(2)}) copy-start(f32[1,512,512]{1,2,0:T(8,128)S(1)} %fusion.1) | copy-start | bytes 3145732
  25.7 25.4 %collective-permute-start.4 = (f32[1,512,512]{1,2,0:T(8,128)S(1)}, f32[1,512,512]{1,2,0:T(8,128)}, u32[]{:S(2)}, u32[]{:S(2)}) collective-permute-start(f32[1,512,512]{1,2,0:T(8,128)S(1)} %fusion.1), channel_id=1, source_target_pairs={{0,16},{16,0},{1,17},{17,1},{2,18},{18,2},{3,19},{19,3},{4,20},{20... | collective-permute-start | bytes 3145736 | tf_op jit(solution)/shard_map/ppermute | solution.py:22
  66.7 24.5 %collective-permute-start.5 = (f32[512,512]{0,1:T(8,128)S(1)}, f32[512,512]{0,1:T(8,128)}, u32[]{:S(2)}, u32[]{:S(2)}) collective-permute-start(f32[512,512]{0,1:T(8,128)S(1)} %copy.18), channel_id=1, source_target_pairs={{0,16},{16,0},{1,17},{17,1},{2,18},{18,2},{3,19},{19,3},{4,20},{20... | collective-permute-start | bytes 3145736 | tf_op jit(solution)/shard_map/ppermute | solution.py:22
